TPU v7x, 32 devices: a whole 2x2x4 slice. The times are simulated.
32 devices in a mesh: grp: 2 (over y), exp: 4 (over z), tp: 4 (over x, core).
Axes of the slice: x: 2, y: 2, z: 4, core: 2. Of those that a mesh axis runs over, the one named last changes fastest.
Arguments:
- tokens: bfloat16 [128, 3584], P(('grp', 'exp'), 'tp'), parts along dimension 0, may hold values from -6 to 6
- gate_up_weight: bfloat16 [3584, 2, 18944], P('tp', None, 'exp'), may hold values from -0.09375 to 0.09375
- down_weight: bfloat16 [18944, 3584], P('exp', 'tp'), may hold values from -0.046875 to 0.046875
- adapter_in: bfloat16 [4, 3584, 16], P('exp', 'tp'), may hold values from -0.09375 to 0.09375
- adapter_out: bfloat16 [4, 16, 3584], P('exp', None, 'tp'), may hold values from -1.5 to 1.5
- expert_ids: int32 [128, 2], P(('grp', 'exp')), parts along dimension 0, may hold values from 0 to 3, all different within a row; in each aligned block of 16 rows (0 to 15, 16 to 31, ...) at most 16 rows name the same one
- route_weight: float32 [128, 2], P(('grp', 'exp')), parts along dimension 0, may hold values from 0.2 to 1
Outputs:
- mixed: bfloat16 [128, 3584], P(('grp', 'exp'), 'tp'), parts along dimension 0
There are 2 independent parts, one for each index of `grp`. A program takes and returns all parts, laid end to end along the dimension named above; an argument that names none is the same for every part. Nothing has to cross between parts.
Inputs may be any that keep to these rules, and one draw needn't show every extreme that they name: `expert_ids`: each row names 2 different experts. Among the 16 rows of one index of exp (aligned blocks of 16 rows) no expert is named by more than 16 rows, and in every draw some expert is named by exactly 16 rows of some block.
All inputs are finite; a program needn't handle non-finite values.
Results may differ from a plain program's by a relative error of at most 0.025.
Values may be sent and summed in bfloat16 or wider, within the bound.
A program may use at most 64 MiB of HBM per device.

v0:
```python
import functools
import jax
import jax.numpy as jnp
from jax import lax
from jax.experimental import pallas as pl
from jax.experimental.pallas import tpu as pltpu
from jax.sharding import PartitionSpec as P

LANES = 128
CHUNK_TILES = 6
STEP_TILES = 6
RELAY_LAG = 6
MESH = pl.DeviceIdType.MESH
BF16, F32 = jnp.bfloat16, jnp.float32


def chunks_of(tiles):
    spans, first = [], 0
    while first < tiles:
        count = min(CHUNK_TILES, tiles - first)
        spans.append((first, count))
        first += count
    return spans


def kernel(
    exp_count, tok_ref, gu_ref, down_ref, ain_ref, aout_ref, ids_ref, weight_ref, out_ref,
    gu, down, tok_all, coef_all, coef_own, lhs, ain_pad, aout_pad,
    keep1, send1, recv1, keep2, send2, recv2, hid, total, send_f, recv_f,
    gu_sem, down_sem, tok_send, tok_recv, coef_send, coef_recv,
    s1_send, s1_recv, s2_send, s2_recv, hp_send, hp_recv, hx_send, hx_recv, hr_send, hr_recv,
    f_send, f_recv,
):
    me = lax.axis_index("exp")
    tp = lax.axis_index("tp")
    own_rows, feat = tok_ref.shape
    hidden = gu_ref.shape[2]
    rank = ain_ref.shape[1]
    tiles = hidden // LANES
    spans = chunks_of(tiles)
    core, side = tp % 2, tp // 2
    partner = side * 2 + (1 - core)
    across = (1 - side) * 2 + core
    blocks = [
        core * 2 + side,
        core * 2 + (1 - side),
        (1 - core) * 2 + side,
        (1 - core) * 2 + (1 - side),
    ]
    mine, crossed = blocks[0], blocks[1]

    gu_flat = gu_ref.reshape(2 * feat, hidden)

    def gu_copy(t):
        cols = pl.ds(pl.multiple_of(t * LANES, LANES), LANES)
        return pltpu.make_async_copy(gu_flat.at[:, cols], gu.at[t], gu_sem.at[t])

    def down_copy(j):
        first, count = spans[j]
        rows = pl.ds(first * LANES, count * LANES)
        return pltpu.make_async_copy(down_ref.at[rows], down.at[rows], down_sem.at[j])

    def start_gu(t, carry):
        gu_copy(t).start()
        return carry

    lax.fori_loop(0, tiles, start_gu, 0)
    for j in range(len(spans)):
        down_copy(j).start()

    barrier = pltpu.get_barrier_semaphore()
    for d in range(1, exp_count):
        pl.semaphore_signal(
            barrier, inc=1, device_id={"exp": (me + d) % exp_count}, device_id_type=MESH
        )
    for peer in (partner, across):
        pl.semaphore_signal(barrier, inc=1, device_id={"tp": peer}, device_id_type=MESH)

    lane = lax.broadcasted_iota(jnp.int32, (own_rows, LANES), 1)
    diagonal = lax.broadcasted_iota(
        jnp.int32, (own_rows, own_rows), 0
    ) == lax.broadcasted_iota(jnp.int32, (own_rows, own_rows), 1)

    def column_of(line):
        return jnp.sum(jnp.where(diagonal, line, 0.0), axis=1, keepdims=True)

    coef = jnp.zeros((own_rows, LANES), F32)
    for k in range(ids_ref.shape[0]):
        named = column_of(ids_ref[k:k + 1, :].astype(F32)).astype(jnp.int32)
        coef = coef + jnp.where(lane == named, column_of(weight_ref[k:k + 1, :]), 0.0)
    coef_own[...] = coef
    coef_all[me] = coef
    tok_all[me] = tok_ref[...]
    ain_pad[...] = jnp.zeros_like(ain_pad)
    ain_pad[:rank, :] = ain_ref[0]
    aout_pad[...] = jnp.zeros_like(aout_pad)
    aout_pad[:rank, :] = aout_ref[0]

    pl.semaphore_wait(barrier, exp_count + 1)

    def exp_copy(src, dst, send, recv, d):
        return pltpu.make_async_remote_copy(
            src_ref=src, dst_ref=dst, send_sem=send.at[d - 1], recv_sem=recv.at[d - 1],
            device_id={"exp": (me + d) % exp_count}, device_id_type=MESH,
        )

    tok_copies = [
        exp_copy(tok_ref, tok_all.at[me], tok_send, tok_recv, d) for d in range(1, exp_count)
    ]
    coef_copies = [
        exp_copy(coef_own, coef_all.at[me], coef_send, coef_recv, d) for d in range(1, exp_count)
    ]
    for copy in tok_copies + coef_copies:
        copy.start()

    def span_cols(j):
        first, count = spans[j]
        if j == 0:
            return pl.ds(0, (count + 1) * LANES)
        return pl.ds((first + 1) * LANES, count * LANES)

    def tp_copy(src, dst, send, recv, j, peer):
        return pltpu.make_async_remote_copy(
            src_ref=src, dst_ref=dst, send_sem=send.at[j], recv_sem=recv.at[j],
            device_id={"tp": peer}, device_id_type=MESH,
        )

    def s1_copy(j):
        cols = span_cols(j)
        return tp_copy(send1.at[:, cols], recv1.at[:, cols], s1_send, s1_recv, j, partner)

    def s2_copy(j):
        cols = span_cols(j)
        return tp_copy(send2.at[:, cols], recv2.at[:, cols], s2_send, s2_recv, j, across)

    def hp_copy(j):
        ref = hid.at[mine, :, span_cols(j)]
        return tp_copy(ref, ref, hp_send, hp_recv, j, partner)

    def hx_copy(j):
        ref = hid.at[mine, :, span_cols(j)]
        return tp_copy(ref, ref, hx_send, hx_recv, j, across)

    def hr_copy(j):
        ref = hid.at[crossed, :, span_cols(j)]
        return tp_copy(ref, ref, hr_send, hr_recv, j, partner)

    for copy in tok_copies:
        copy.wait_recv()

    row = lax.broadcasted_iota(jnp.int32, (LANES, 4 * LANES), 0)
    col = lax.broadcasted_iota(jnp.int32, (LANES, 4 * LANES), 1)
    spread = jnp.where(col % (2 * LANES) == 2 * row + col // (2 * LANES), 1.0, 0.0).astype(BF16)
    ordered = jnp.concatenate([tok_all[b] for b in blocks], axis=0)
    rows = ordered.shape[0]
    stacked = jnp.concatenate(
        [ordered[:, k * LANES:(k + 1) * LANES] for k in range(feat // LANES)], axis=0
    )
    wide = jnp.dot(stacked, spread, preferred_element_type=F32).astype(BF16)
    for k in range(feat // LANES):
        for p in range(4):
            for s in range(2):
                lhs[
                    (2 * p + s) * own_rows:(2 * p + s + 1) * own_rows,
                    2 * k * LANES:2 * (k + 1) * LANES,
                ] = wide[
                    k * rows + p * own_rows:k * rows + (p + 1) * own_rows,
                    2 * s * LANES:2 * (s + 1) * LANES,
                ]

    half = 4 * own_rows

    def store_pair(cols, value):
        keep1[:, cols] = value[:half]
        send1[:, cols] = value[half:].astype(BF16)

    def product(j):
        first, count = spans[j]

        def several(t, width):
            for i in range(width):
                gu_copy(t + i).wait()
            weight = jnp.concatenate([gu[t + i] for i in range(width)], axis=1)
            value = jnp.dot(lhs[...], weight, preferred_element_type=F32)
            store_pair(pl.ds(pl.multiple_of((t + 1) * LANES, LANES), width * LANES), value)

        def step(i, carry):
            several(first + STEP_TILES * i, STEP_TILES)
            return carry

        lax.fori_loop(0, count // STEP_TILES, step, 0)
        if count % STEP_TILES:
            several(first + count - count % STEP_TILES, count % STEP_TILES)
        s1_copy(j).start()

    def rank_product():
        value = lax.dot_general(
            ordered, ain_pad[...], (((1,), (1,)), ((), ())), preferred_element_type=F32
        )
        blank = jnp.zeros((own_rows, LANES), F32)
        parts = []
        for p in range(4):
            parts += [value[p * own_rows:(p + 1) * own_rows], blank]
        store_pair(pl.ds(0, LANES), jnp.concatenate(parts, axis=0))

    def reduce_near(j):
        s1_copy(j).wait_recv()
        cols = span_cols(j)
        value = keep1[:, cols] + recv1[:, cols].astype(F32)
        keep2[:, cols] = value[:2 * own_rows]
        send2[:, cols] = value[2 * own_rows:].astype(BF16)
        s2_copy(j).start()

    def activate(j):
        s2_copy(j).wait_recv()
        first, count = spans[j]
        cols = pl.ds((first + 1) * LANES, count * LANES)
        pair = keep2[:, cols] + recv2[:, cols].astype(F32)
        hid[mine, :, cols] = (jax.nn.silu(pair[:own_rows]) * pair[own_rows:]).astype(BF16)
        if j == 0:
            cols = pl.ds(0, LANES)
            pair = keep2[:own_rows, cols] + recv2[:own_rows, cols].astype(F32)
            hid[mine, :, cols] = pair.astype(BF16)
        hx_copy(j).start()
        hp_copy(j).start()

    def relay(j):
        hx_copy(j).wait_recv()
        hr_copy(j).start()

    def adapter_part():
        for copy in coef_copies:
            copy.wait_recv()
        rank_mid = hid[:, :, pl.ds(0, LANES)].reshape(rows, LANES)
        expert_out = jnp.dot(rank_mid, aout_pad[...], preferred_element_type=F32).astype(BF16)
        all_coef = coef_all[...].reshape(rows, LANES)
        wide_lane = lax.broadcasted_iota(jnp.int32, (rows, LANES), 1)
        column = jnp.sum(jnp.where(wide_lane == me, all_coef, 0.0), axis=1, keepdims=True)
        return column * expert_out.astype(F32)

    def project(j):
        hp_copy(j).wait_recv()
        hr_copy(j).wait_recv()
        down_copy(j).wait()
        first, count = spans[j]
        cols = pl.ds((first + 1) * LANES, count * LANES)
        value = jnp.dot(
            hid[:, :, cols].reshape(rows, count * LANES),
            down[pl.ds(first * LANES, count * LANES), :],
            preferred_element_type=F32,
        )
        if j == 0:
            total[...] = value + adapter_part()
        else:
            total[...] += value

    chunk_count = len(spans)
    stages = (
        (product, 0), (reduce_near, 1), (activate, 4), (relay, RELAY_LAG), (project, RELAY_LAG + 1),
    )
    rank_product()
    for step in range(chunk_count + RELAY_LAG + 1):
        for stage, lag in stages:
            if 0 <= step - lag < chunk_count:
                stage(step - lag)

    part = total[...]
    send_f[...] = part.astype(BF16).reshape(exp_count, own_rows, feat)
    f_copies = [
        exp_copy(send_f.at[(me + d) % exp_count], recv_f.at[d - 1], f_send, f_recv, d)
        for d in range(1, exp_count)
    ]
    for copy in f_copies:
        copy.start()
    result = total[pl.ds(pl.multiple_of(me * own_rows, own_rows), own_rows), :]
    for copy, d in zip(f_copies, range(1, exp_count)):
        copy.wait_recv()
        result = result + recv_f[d - 1].astype(F32)
    out_ref[...] = result.astype(out_ref.dtype)

    for copy in tok_copies + coef_copies + f_copies:
        copy.wait_send()
    for j in range(chunk_count):
        for make in (s1_copy, s2_copy, hp_copy, hx_copy, hr_copy):
            make(j).wait_send()


def fused(tokens, gate_up_weight, down_weight, adapter_in, adapter_out, expert_ids, route_weight):
    exp_count = lax.axis_size("exp")
    own_rows, feat = tokens.shape
    hidden = gate_up_weight.shape[2]
    tiles = hidden // LANES
    chunk_count = len(chunks_of(tiles))
    wide = hidden + LANES
    rows = exp_count * own_rows
    vmem = functools.partial(pltpu.VMEM)
    dma = lambda n: pltpu.SemaphoreType.DMA((n,))
    peers = exp_count - 1
    in_vmem = pl.BlockSpec(memory_space=pltpu.VMEM)
    in_place = pl.BlockSpec(memory_space=pl.ANY)
    return pl.pallas_call(
        functools.partial(kernel, exp_count),
        out_shape=jax.ShapeDtypeStruct((own_rows, feat), BF16),
        in_specs=[in_vmem, in_place, in_place, in_vmem, in_vmem, in_vmem, in_vmem],
        out_specs=in_vmem,
        scratch_shapes=[
            vmem((tiles, 2 * feat, LANES), BF16),
            vmem((hidden, feat), BF16),
            vmem((exp_count, own_rows, feat), BF16),
            vmem((exp_count, own_rows, LANES), F32),
            vmem((own_rows, LANES), F32),
            vmem((2 * rows, 2 * feat), BF16),
            vmem((LANES, feat), BF16),
            vmem((LANES, feat), BF16),
            vmem((4 * own_rows, wide), F32),
            vmem((4 * own_rows, wide), BF16),
            vmem((4 * own_rows, wide), BF16),
            vmem((2 * own_rows, wide), F32),
            vmem((2 * own_rows, wide), BF16),
            vmem((2 * own_rows, wide), BF16),
            vmem((4, own_rows, wide), BF16),
            vmem((rows, feat), F32),
            vmem((exp_count, own_rows, feat), BF16),
            vmem((peers, own_rows, feat), BF16),
            dma(tiles), dma(chunk_count),
            dma(peers), dma(peers), dma(peers), dma(peers),
            *[dma(chunk_count) for _ in range(10)],
            dma(peers), dma(peers),
        ],
        compiler_params=pltpu.CompilerParams(
            collective_id=0, has_side_effects=True, vmem_limit_bytes=60 * 2**20
        ),
    )(
        tokens, gate_up_weight, down_weight, jnp.swapaxes(adapter_in, 1, 2), adapter_out,
        expert_ids.T, route_weight.T,
    )


def plain(tokens, gate_up_weight, down_weight, adapter_in, adapter_out, expert_ids, route_weight):
    exp_count = lax.axis_size("exp")
    own_rows, feat_width = tokens.shape
    all_tokens = lax.all_gather(tokens, "exp", axis=0, tiled=True)
    hidden_width = gate_up_weight.shape[2]
    pair_weight = gate_up_weight.reshape(feat_width, 2 * hidden_width)
    pair_share = lax.psum_scatter(
        jnp.dot(all_tokens, pair_weight, preferred_element_type=jnp.float32).astype(jnp.bfloat16),
        "tp",
        scatter_dimension=0,
        tiled=True,
    ).astype(jnp.float32)
    hidden_share = (
        jax.nn.silu(pair_share[:, :hidden_width]) * pair_share[:, hidden_width:]
    ).astype(jnp.bfloat16)
    hidden = lax.all_gather(hidden_share, "tp", axis=0, tiled=True)
    base_out = lax.psum_scatter(
        jnp.dot(hidden, down_weight, preferred_element_type=jnp.float32).astype(jnp.bfloat16),
        "exp",
        scatter_dimension=0,
        tiled=True,
    ).astype(jnp.float32)
    top_count = expert_ids.shape[1]
    expert_count = adapter_in.shape[0] * exp_count
    flat_ids = expert_ids.reshape(own_rows * top_count)
    flat_weight = route_weight.reshape(own_rows * top_count)
    expert_hits = (flat_ids[:, None] == jnp.arange(expert_count, dtype=jnp.int32)[None, :]).astype(
        jnp.int32
    )
    capacity = max(2, 2 * top_count * own_rows // expert_count)
    slot_index = jnp.sum((jnp.cumsum(expert_hits, axis=0) - expert_hits) * expert_hits, axis=1)
    slot_target = flat_ids * capacity + slot_index
    slot_hits = (
        slot_target[:, None] == jnp.arange(expert_count * capacity, dtype=jnp.int32)[None, :]
    )
    combine_matrix = jnp.sum(
        (slot_hits.astype(jnp.float32) * flat_weight[:, None]).reshape(
            own_rows, top_count, expert_count * capacity
        ),
        axis=1,
    )
    dispatch_matrix = slot_hits.T.astype(jnp.bfloat16)
    repeated = jnp.repeat(tokens, top_count, axis=0)
    outgoing = jnp.dot(dispatch_matrix, repeated, preferred_element_type=jnp.float32).astype(
        jnp.bfloat16
    )
    outgoing = outgoing.reshape(expert_count, capacity, feat_width)
    rank_partial = jnp.einsum(
        "scd,dr->scr",
        lax.all_to_all(outgoing, "exp", split_axis=0, concat_axis=0, tiled=True),
        adapter_in[0],
        preferred_element_type=jnp.float32,
    )
    rank_mid = lax.psum(rank_partial, "tp").astype(jnp.bfloat16)
    expert_out = jnp.einsum(
        "scr,rd->scd", rank_mid, adapter_out[0], preferred_element_type=jnp.float32
    ).astype(jnp.bfloat16)
    returned = lax.all_to_all(expert_out, "exp", split_axis=0, concat_axis=0, tiled=True)
    adapter_sum = jnp.dot(
        combine_matrix,
        returned.reshape(expert_count * capacity, feat_width).astype(jnp.float32),
        precision=lax.Precision.HIGHEST,
        preferred_element_type=jnp.float32,
    )
    return (base_out + adapter_sum).astype(jnp.bfloat16)


def local(tokens, gate_up_weight, *rest):
    own_rows, feat = tokens.shape
    fits = (
        lax.axis_size("tp") == 4
        and lax.axis_size("exp") == 4
        and rest[1].shape[0] == 1
        and rest[1].shape[2] <= LANES
        and own_rows % 16 == 0
        and feat % LANES == 0
        and gate_up_weight.shape[2] % LANES == 0
    )
    return (fused if fits else plain)(tokens, gate_up_weight, *rest)


def solution(mesh):
    in_specs = (
        P(("grp", "exp"), "tp"),
        P("tp", None, "exp"),
        P("exp", "tp"),
        P("exp", "tp", None),
        P("exp", None, "tp"),
        P(("grp", "exp"), None),
        P(("grp", "exp"), None),
    )
    out_specs = P(("grp", "exp"), "tp")
    return jax.shard_map(local, mesh=mesh, in_specs=in_specs, out_specs=out_specs, check_vma=False)
```

profile of v0, /device:TPU:0, one launch (start us, length us, event | category | flops | bytes accessed | tf_op | source)
XLA Modules:
  0.0 34.7 jit_solution(1198749876875907179)
XLA Ops:
  0.0 33.3 %shard_map.73 = bf16[16,896]{1,0:T(8,128)(2,1)} custom-call(bf16[16,896]{1,0:T(8,128)(2,1)} %tok_ref.1, bf16[896,2,4736]{2,1,0:T(2,128)(2,1)} %gu_ref.1, bf16[4736,896]{1,0:T(8,128)(2,1)} %down_ref.1, bf16[1,16,896]{2,1,0:T(8,128)(2,1)} %bitcast.3, bf16[1,16,896]{2,1,0:T(8,128)(2,1)} %aout_ref.1, s32[2,16]{1,0:T(2,128)} %bitcast.4, f32[2,16]{1,0:T(2,128)} %bitcast.5), custom_call_target="tpu_custom_call" | custom-call | tf_op jit(solution)/shard_map/pallas_call | solution.py:301
  33.3 1.4 %copy.9 = bf16[16,896]{1,0:T(8,128)(2,1)} copy(bf16[16,896]{1,0:T(8,128)(2,1)} %shard_map.73) | data formatting | bytes 57344
where the time goes:
time: 34.9 us; the launch traced here: 34.7 us
  Pallas kernels  33.3 us (95%)
  local copies, waits for them, and re-layouts  1.36 us (4%)
    pallas_call x1, Pallas kernels, fused(): pl.pallas_call(functools.partial(kernel, exp_count), out_shape=jax.ShapeD...  33.3 us
    unnamed x1, local copies, waits for them, and re-layouts  1.36 us

commit v1 on v0

v1 whole, which is shorter than its diff:
```python
import functools
import jax
import jax.numpy as jnp
from jax import lax
from jax.experimental import pallas as pl
from jax.experimental.pallas import tpu as pltpu
from jax.sharding import PartitionSpec as P

LANES = 128
CHUNK_TILES = 6
EARLY_CHUNKS = 3
MESH = pl.DeviceIdType.MESH
BF16, F32 = jnp.bfloat16, jnp.float32
NEAR, FAR = 0, 1

NEAR_READY, FAR_READY = 4.2, 6.0
LOAD_START, LOAD_TILE = 0.9, 0.135
DOT_BASE, DOT_TILE = 0.15, 0.083
DOWN_BASE, DOWN_TILE = 0.12, 0.04
PARTNER_DELAY, ACROSS_DELAY = 1.05, 2.3
ACROSS_HALF_TILE = 0.088


def chunks_of(columns):
    spans, first = [], 0
    while first < columns:
        count = min(CHUNK_TILES, columns - first)
        spans.append((first, count))
        first += count
    return spans


def plan(spans):
    count = len(spans)
    early = min(EARLY_CHUNKS, count)
    rank = {}
    for s, chunks in ((NEAR, range(early)), (FAR, range(count)), (NEAR, range(early, count))):
        for j in chunks:
            rank[s, j] = len(rank)
    products = [((NEAR,), j) for j in range(early)] + [((FAR,), j) for j in range(early)]
    products += [((FAR, NEAR), j) for j in range(early, count)]
    ready = {}
    pending_down = [((NEAR, FAR), j) for j in range(early)]
    pending_down += [((FAR,), j) for j in range(early, count)]
    pending_down += [((NEAR,), j) for j in range(early, count)]
    now, link, order = 0.0, 0.0, []
    loaded = lambda j: LOAD_START + LOAD_TILE * (spans[j][0] + spans[j][1])
    waiting = []

    def send(j, tiles_half):
        nonlocal link
        link = max(link, now) + ACROSS_HALF_TILE * tiles_half
        return link + ACROSS_DELAY

    far_left = count
    near_left = count
    while products or waiting or pending_down:
        options = []
        for name, s, j in waiting:
            options.append((ready[name, s, j], (0 if name != "relay" else 1, rank[s, j]), (name, s, j)))
        if products:
            sets, j = products[0]
            at = max(loaded(j), max(NEAR_READY if s == NEAR else FAR_READY for s in sets))
            options.append((at, (2, 0), ("product", sets, j)))
        for sets, j in pending_down:
            at = [ready.get(("project", s, j)) for s in sets]
            if None not in at:
                place = 3 if sets != (FAR,) else 2
                options.append((max(at), (place, rank[sets[-1], j]), ("project", sets, j)))
        able = [o for o in options if o[0] <= now + 0.02]
        pick = min(able, key=lambda o: o[1]) if able else min(options)
        now = max(now, pick[0])
        name, s, j = pick[2]
        order.append(pick[2])
        half = spans[j][1] / 2
        if name == "product":
            products.pop(0)
            now += DOT_BASE + DOT_TILE * spans[j][1]
            for one in s:
                waiting.append(("reduce", one, j))
                ready["reduce", one, j] = now + PARTNER_DELAY
        elif name == "project":
            pending_down.remove((s, j))
            now += DOWN_BASE + DOWN_TILE * spans[j][1]
            if FAR in s:
                far_left -= 1
                if far_left == 0:
                    order.append(("finish", FAR, 0))
            if NEAR in s:
                near_left -= 1
                if near_left == 0:
                    order.append(("finish", NEAR, 0))
        else:
            waiting.remove(pick[2])
            now += 0.03
            if name == "reduce":
                waiting.append(("activate", s, j))
                ready["activate", s, j] = send(j, 2 * half)
            elif name == "activate":
                waiting.append(("relay", s, j))
                ready["relay", s, j] = send(j, half)
            else:
                ready["project", s, j] = now + PARTNER_DELAY
    return order


def kernel(
    tok_ref, gu_ref, down_ref, ain_ref, aout_ref, ids_ref, weight_ref, out_ref,
    gu, down, tok_all, ain_pad, aout_pad, ids, weights, coef_own, coef_all, lhs,
    keep1, send1, recv1, keep2, send2, recv2, hid, total, send_f, recv_f,
    gu_sem, down_sem, in_sem, tok_send, tok_recv, coef_send, coef_recv,
    s1_send, s1_recv, s2_send, s2_recv, hp_send, hp_recv, hx_send, hx_recv, hr_send, hr_recv,
    f_send, f_recv,
):
    me = lax.axis_index("exp")
    tp = lax.axis_index("tp")
    own_rows, feat = tok_ref.shape
    hidden = gu_ref.shape[2]
    rank = ain_ref.shape[1]
    tiles = hidden // LANES
    spans = chunks_of(tiles + 1)
    core, side = tp % 2, tp // 2
    partner = side * 2 + (1 - core)
    across = (1 - side) * 2 + core
    low = me - me % 2
    lows = (low, (low + 2) % 4)
    near = low + 1 - me % 2
    far = (me + 2) % 4
    peers = (near, far, (near + 2) % 4)

    barrier = pltpu.get_barrier_semaphore()
    for peer in peers:
        pl.semaphore_signal(barrier, inc=1, device_id={"exp": peer}, device_id_type=MESH)
    for peer in (partner, across):
        pl.semaphore_signal(barrier, inc=1, device_id={"tp": peer}, device_id_type=MESH)

    in_copies = [
        pltpu.make_async_copy(tok_ref, tok_all.at[me], in_sem.at[0]),
        pltpu.make_async_copy(ids_ref, ids, in_sem.at[1]),
        pltpu.make_async_copy(weight_ref, weights, in_sem.at[2]),
        pltpu.make_async_copy(ain_ref.at[0], ain_pad.at[pl.ds(0, rank)], in_sem.at[3]),
        pltpu.make_async_copy(aout_ref.at[0], aout_pad.at[pl.ds(0, rank)], in_sem.at[4]),
    ]
    gu_flat = gu_ref.reshape(2 * feat, hidden)

    def gu_copy(t):
        cols = pl.ds(pl.multiple_of(t * LANES, LANES), LANES)
        return pltpu.make_async_copy(gu_flat.at[:, cols], gu.at[t], gu_sem.at[t])

    def down_rows(j):
        first, count = spans[j]
        begin, end = max(first - 1, 0), first + count - 1
        return pl.ds(begin * LANES, (end - begin) * LANES)

    def down_copy(j):
        rows = down_rows(j)
        return pltpu.make_async_copy(down_ref.at[rows], down.at[rows], down_sem.at[j])

    for copy in in_copies:
        copy.start()

    def start_gu(t, carry):
        gu_copy(t).start()
        return carry

    lax.fori_loop(0, tiles, start_gu, 0)
    for j in range(len(spans)):
        down_copy(j).start()

    ain_pad[rank:, :] = jnp.zeros((LANES - rank, feat), BF16)
    aout_pad[rank:, :] = jnp.zeros((LANES - rank, feat), BF16)

    def exp_copy(src, dst, send, recv, r):
        return pltpu.make_async_remote_copy(
            src_ref=src, dst_ref=dst, send_sem=send.at[r], recv_sem=recv.at[r],
            device_id={"exp": peers[r]}, device_id_type=MESH,
        )

    tok_copies = [
        exp_copy(tok_all.at[me], tok_all.at[me], tok_send, tok_recv, r) for r in range(3)
    ]
    coef_copies = [
        exp_copy(coef_own.at[r], coef_all.at[me], coef_send, coef_recv, r) for r in range(3)
    ]
    in_copies[1].wait()
    in_copies[2].wait()

    def coef_line(expert):
        line = jnp.zeros((1, own_rows), F32)
        for k in range(ids.shape[0]):
            line = line + jnp.where(ids[k:k + 1, :] == expert, weights[k:k + 1, :], 0.0)
        return jnp.concatenate([line, jnp.zeros((1, LANES - own_rows), F32)], axis=1)

    for r in range(3):
        coef_own[r, 0:1, :] = coef_line(peers[r])
    coef_all[me, 0:1, :] = coef_line(me)
    in_copies[0].wait()

    pl.semaphore_wait(barrier, 5)
    for copy in tok_copies + coef_copies:
        copy.start()

    def span_cols(j):
        first, count = spans[j]
        return pl.ds(first * LANES, count * LANES)

    def half_cols(j, which):
        first, count = spans[j]
        width = count // 2 * LANES
        return pl.ds(pl.multiple_of(first * LANES + which * width, LANES), width)

    def pack_cols(j):
        first, count = spans[j]
        return pl.ds(first // 2 * LANES, count // 2 * LANES)

    def tp_copy(src, dst, send, recv, s, j, peer):
        return pltpu.make_async_remote_copy(
            src_ref=src, dst_ref=dst, send_sem=send.at[s, j], recv_sem=recv.at[s, j],
            device_id={"tp": peer}, device_id_type=MESH,
        )

    def s1_copy(s, j):
        cols = span_cols(j)
        return tp_copy(
            send1.at[s, :, cols], recv1.at[s, :, cols], s1_send, s1_recv, s, j, partner
        )

    def s2_copy(s, j):
        cols = pack_cols(j)
        return tp_copy(
            send2.at[s, :, cols], recv2.at[s, :, cols], s2_send, s2_recv, s, j, across
        )

    def hp_copy(s, j):
        ref = hid.at[s, core, :, half_cols(j, side)]
        return tp_copy(ref, ref, hp_send, hp_recv, s, j, partner)

    def hx_copy(s, j):
        ref = hid.at[s, core, :, half_cols(j, side)]
        return tp_copy(ref, ref, hx_send, hx_recv, s, j, across)

    def hr_copy(s, j):
        ref = hid.at[s, core, :, half_cols(j, 1 - side)]
        return tp_copy(ref, ref, hr_send, hr_recv, s, j, partner)

    pair_rows = 2 * own_rows
    row = lax.broadcasted_iota(jnp.int32, (LANES, 4 * LANES), 0)
    col = lax.broadcasted_iota(jnp.int32, (LANES, 4 * LANES), 1)
    spread = jnp.where(col % (2 * LANES) == 2 * row + col // (2 * LANES), 1.0, 0.0).astype(BF16)

    def ordered(s):
        return jnp.concatenate([tok_all[lows[s] + core], tok_all[lows[s] + 1 - core]], axis=0)

    def prepare(s):
        for r in ((0,) if s == NEAR else (1, 2)):
            tok_copies[r].wait_recv()
        tokens = ordered(s)
        stacked = jnp.concatenate(
            [tokens[:, k * LANES:(k + 1) * LANES] for k in range(feat // LANES)], axis=0
        )
        wide = jnp.dot(stacked, spread, preferred_element_type=F32).astype(BF16)
        for k in range(feat // LANES):
            for p in range(2):
                for half in range(2):
                    to = 2 * s * pair_rows + (2 * p + half) * own_rows
                    lhs[to:to + own_rows, 2 * k * LANES:2 * (k + 1) * LANES] = wide[
                        k * pair_rows + p * own_rows:k * pair_rows + (p + 1) * own_rows,
                        2 * half * LANES:2 * (half + 1) * LANES,
                    ]
        if s == NEAR:
            in_copies[3].wait()
        value = lax.dot_general(
            tokens, ain_pad[...], (((1,), (1,)), ((), ())), preferred_element_type=F32
        )
        blank = jnp.zeros((own_rows, LANES), F32)
        store_pair(
            s, pl.ds(0, LANES),
            jnp.concatenate([value[:own_rows], blank, value[own_rows:], blank], axis=0),
        )

    def store_pair(s, cols, value):
        keep1[s, :, cols] = value[:pair_rows]
        send1[s, :, cols] = value[pair_rows:].astype(BF16)

    arrived = set()

    def product(sets, j):
        for s in sets:
            if s not in arrived:
                arrived.add(s)
                prepare(s)
        first, count = spans[j]
        begin, end = max(first - 1, 0), first + count - 1
        for t in range(begin, end):
            if ("gu", t) not in arrived:
                arrived.add(("gu", t))
                gu_copy(t).wait()
        weight = jnp.concatenate([gu[t] for t in range(begin, end)], axis=1)
        rows = slice(0, 4 * pair_rows) if len(sets) == 2 else slice(
            2 * sets[0] * pair_rows, 2 * (sets[0] + 1) * pair_rows
        )
        value = jnp.dot(lhs[rows, :], weight, preferred_element_type=F32)
        cols = pl.ds((begin + 1) * LANES, (end - begin) * LANES)
        for s in sets:
            at = 2 * s * pair_rows if len(sets) == 2 else 0
            store_pair(s, cols, value[at:at + 2 * pair_rows])
            s1_copy(s, j).start()

    def reduce(s, j):
        s1_copy(s, j).wait_recv()
        cols = pack_cols(j)
        kept, sent = half_cols(j, side), half_cols(j, 1 - side)
        send2[s, :, cols] = (keep1[s, :, sent] + recv1[s, :, sent].astype(F32)).astype(BF16)
        s2_copy(s, j).start()
        keep2[s, :, cols] = keep1[s, :, kept] + recv1[s, :, kept].astype(F32)

    def activate(s, j):
        s2_copy(s, j).wait_recv()
        cols = pack_cols(j)
        pair = keep2[s, :, cols] + recv2[s, :, cols].astype(F32)
        value = jax.nn.silu(pair[:own_rows]) * pair[own_rows:]
        if j == 0:
            first = jnp.where(side == 0, pair[:own_rows, :LANES], value[:, :LANES])
            value = jnp.concatenate([first, value[:, LANES:]], axis=1)
        hid[s, core, :, half_cols(j, side)] = value.astype(BF16)
        hx_copy(s, j).start()
        hp_copy(s, j).start()

    def relay(s, j):
        hx_copy(s, j).wait_recv()
        hr_copy(s, j).start()

    diagonal = lax.broadcasted_iota(
        jnp.int32, (own_rows, own_rows), 0
    ) == lax.broadcasted_iota(jnp.int32, (own_rows, own_rows), 1)

    def adapter_part(s):
        if s == NEAR:
            in_copies[4].wait()
        for r in ((0,) if s == NEAR else (1, 2)):
            coef_copies[r].wait_recv()
        rank_mid = hid[s, :, :, pl.ds(0, LANES)].reshape(pair_rows, LANES)
        expert_out = jnp.dot(rank_mid, aout_pad[...], preferred_element_type=F32).astype(BF16)
        columns = []
        for c in range(2):
            line = coef_all[lows[s] + c, 0:1, :][:, :own_rows]
            columns.append(jnp.sum(jnp.where(diagonal, line, 0.0), axis=1, keepdims=True))
        return jnp.concatenate(columns, axis=0) * expert_out.astype(F32)

    def project(sets, j):
        for s in sets:
            hp_copy(s, j).wait_recv()
            hr_copy(s, j).wait_recv()
        if ("down", j) not in arrived:
            arrived.add(("down", j))
            down_copy(j).wait()
        first, count = spans[j]
        begin, end = max(first, 1), first + count
        cols = pl.ds(begin * LANES, (end - begin) * LANES)
        units = jnp.concatenate(
            [hid[s, :, :, cols].reshape(pair_rows, (end - begin) * LANES) for s in sets], axis=0
        )
        value = jnp.dot(units, down[down_rows(j), :], preferred_element_type=F32)
        for i, s in enumerate(sets):
            part = value[i * pair_rows:(i + 1) * pair_rows]
            if j == 0:
                part = part + adapter_part(s)
            if ("total", s) not in arrived:
                arrived.add(("total", s))
                total[s] = part
            else:
                total[s] += part

    def f_copy(r):
        return exp_copy(send_f.at[r], recv_f.at[r], f_send, f_recv, r)

    def finish(s, j):
        for r in ((0,) if s == NEAR else (1, 2)):
            at = pl.ds(pl.multiple_of(peers[r] % 2 * own_rows, own_rows), own_rows)
            send_f[r] = total[s, at, :].astype(BF16)
            f_copy(r).start()

    stages = {
        "product": product, "reduce": reduce, "activate": activate, "relay": relay,
        "project": project, "finish": finish,
    }
    for name, s, j in plan(spans):
        with jax.named_scope(f"{name}{s}{j}"):
            stages[name](s, j)

    with jax.named_scope("sends"):
        for copy in tok_copies + coef_copies:
            copy.wait_send()
        for s in range(2):
            for j in range(len(spans)):
                for make in (s1_copy, s2_copy, hp_copy, hx_copy, hr_copy):
                    make(s, j).wait_send()
    own = pl.ds(pl.multiple_of(me % 2 * own_rows, own_rows), own_rows)
    result = total[NEAR, own, :]
    for r in (1, 2, 0):
        with jax.named_scope(f"final{r}"):
            f_copy(r).wait_recv()
        result = result + recv_f[r].astype(F32)
    out_ref[...] = result.astype(out_ref.dtype)
    for r in range(3):
        f_copy(r).wait_send()


def fused(tokens, gate_up_weight, down_weight, adapter_in, adapter_out, expert_ids, route_weight):
    own_rows, feat = tokens.shape
    hidden = gate_up_weight.shape[2]
    tiles = hidden // LANES
    chunk_count = len(chunks_of(tiles + 1))
    wide = hidden + LANES
    top = expert_ids.shape[1]
    vmem = pltpu.VMEM
    dma = lambda *shape: pltpu.SemaphoreType.DMA(shape)
    in_place = pl.BlockSpec(memory_space=pltpu.HBM)
    pair = 2 * own_rows
    return pl.pallas_call(
        kernel,
        out_shape=jax.ShapeDtypeStruct((own_rows, feat), BF16),
        in_specs=[in_place] * 7,
        out_specs=pl.BlockSpec(memory_space=pltpu.VMEM),
        scratch_shapes=[
            vmem((tiles, 2 * feat, LANES), BF16),
            vmem((hidden, feat), BF16),
            vmem((4, own_rows, feat), BF16),
            vmem((LANES, feat), BF16),
            vmem((LANES, feat), BF16),
            vmem((top, own_rows), jnp.int32),
            vmem((top, own_rows), F32),
            vmem((3, 8, LANES), F32),
            vmem((4, 8, LANES), F32),
            vmem((4 * pair, 2 * feat), BF16),
            vmem((2, pair, wide), F32),
            vmem((2, pair, wide), BF16),
            vmem((2, pair, wide), BF16),
            vmem((2, pair, wide // 2), F32),
            vmem((2, pair, wide // 2), BF16),
            vmem((2, pair, wide // 2), BF16),
            vmem((2, 2, own_rows, wide), BF16),
            vmem((2, pair, feat), F32),
            vmem((3, own_rows, feat), BF16),
            vmem((3, own_rows, feat), BF16),
            dma(tiles), dma(chunk_count), dma(5),
            dma(3), dma(3), dma(3), dma(3),
            *[dma(2, chunk_count) for _ in range(10)],
            dma(3), dma(3),
        ],
        compiler_params=pltpu.CompilerParams(
            collective_id=0, has_side_effects=True, vmem_limit_bytes=60 * 2**20
        ),
    )(
        tokens, gate_up_weight, down_weight, jnp.swapaxes(adapter_in, 1, 2), adapter_out,
        expert_ids.T, route_weight.T,
    )


def plain(tokens, gate_up_weight, down_weight, adapter_in, adapter_out, expert_ids, route_weight):
    exp_count = lax.axis_size("exp")
    own_rows, feat_width = tokens.shape
    all_tokens = lax.all_gather(tokens, "exp", axis=0, tiled=True)
    hidden_width = gate_up_weight.shape[2]
    pair_weight = gate_up_weight.reshape(feat_width, 2 * hidden_width)
    pair_share = lax.psum_scatter(
        jnp.dot(all_tokens, pair_weight, preferred_element_type=jnp.float32).astype(jnp.bfloat16),
        "tp",
        scatter_dimension=0,
        tiled=True,
    ).astype(jnp.float32)
    hidden_share = (
        jax.nn.silu(pair_share[:, :hidden_width]) * pair_share[:, hidden_width:]
    ).astype(jnp.bfloat16)
    hidden = lax.all_gather(hidden_share, "tp", axis=0, tiled=True)
    base_out = lax.psum_scatter(
        jnp.dot(hidden, down_weight, preferred_element_type=jnp.float32).astype(jnp.bfloat16),
        "exp",
        scatter_dimension=0,
        tiled=True,
    ).astype(jnp.float32)
    top_count = expert_ids.shape[1]
    expert_count = adapter_in.shape[0] * exp_count
    flat_ids = expert_ids.reshape(own_rows * top_count)
    flat_weight = route_weight.reshape(own_rows * top_count)
    expert_hits = (flat_ids[:, None] == jnp.arange(expert_count, dtype=jnp.int32)[None, :]).astype(
        jnp.int32
    )
    capacity = max(2, 2 * top_count * own_rows // expert_count)
    slot_index = jnp.sum((jnp.cumsum(expert_hits, axis=0) - expert_hits) * expert_hits, axis=1)
    slot_target = flat_ids * capacity + slot_index
    slot_hits = (
        slot_target[:, None] == jnp.arange(expert_count * capacity, dtype=jnp.int32)[None, :]
    )
    combine_matrix = jnp.sum(
        (slot_hits.astype(jnp.float32) * flat_weight[:, None]).reshape(
            own_rows, top_count, expert_count * capacity
        ),
        axis=1,
    )
    dispatch_matrix = slot_hits.T.astype(jnp.bfloat16)
    repeated = jnp.repeat(tokens, top_count, axis=0)
    outgoing = jnp.dot(dispatch_matrix, repeated, preferred_element_type=jnp.float32).astype(
        jnp.bfloat16
    )
    outgoing = outgoing.reshape(expert_count, capacity, feat_width)
    rank_partial = jnp.einsum(
        "scd,dr->scr",
        lax.all_to_all(outgoing, "exp", split_axis=0, concat_axis=0, tiled=True),
        adapter_in[0],
        preferred_element_type=jnp.float32,
    )
    rank_mid = lax.psum(rank_partial, "tp").astype(jnp.bfloat16)
    expert_out = jnp.einsum(
        "scr,rd->scd", rank_mid, adapter_out[0], preferred_element_type=jnp.float32
    ).astype(jnp.bfloat16)
    returned = lax.all_to_all(expert_out, "exp", split_axis=0, concat_axis=0, tiled=True)
    adapter_sum = jnp.dot(
        combine_matrix,
        returned.reshape(expert_count * capacity, feat_width).astype(jnp.float32),
        precision=lax.Precision.HIGHEST,
        preferred_element_type=jnp.float32,
    )
    return (base_out + adapter_sum).astype(jnp.bfloat16)


def local(tokens, gate_up_weight, *rest):
    own_rows, feat = tokens.shape
    fits = (
        lax.axis_size("tp") == 4
        and lax.axis_size("exp") == 4
        and rest[1].shape[0] == 1
        and rest[1].shape[2] <= LANES
        and own_rows % 16 == 0
        and feat % LANES == 0
        and gate_up_weight.shape[2] % (2 * LANES) == LANES
    )
    return (fused if fits else plain)(tokens, gate_up_weight, *rest)


def solution(mesh):
    in_specs = (
        P(("grp", "exp"), "tp"),
        P("tp", None, "exp"),
        P("exp", "tp"),
        P("exp", "tp", None),
        P("exp", None, "tp"),
        P(("grp", "exp"), None),
        P(("grp", "exp"), None),
    )
    out_specs = P(("grp", "exp"), "tp")
    return jax.shard_map(local, mesh=mesh, in_specs=in_specs, out_specs=out_specs, check_vma=False)
```

time: 34.9 us -> 33.7 us (0.966)
  Pallas kernels: 33.3 us -> 32.1 us
    pallas_call x1, Pallas kernels: 33.3 us -> 32.1 us  [fused(): pl.pallas_call(kernel, out_shape=jax.ShapeDtypeStruct((own_rows, feat), B...]
where the time goes in v1:
time: 33.7 us; the launch traced here: 33.5 us
  Pallas kernels  32.1 us (95%)
  local copies, waits for them, and re-layouts  1.36 us (4%)
    pallas_call x1, Pallas kernels, fused(): pl.pallas_call(kernel, out_shape=jax.ShapeDtypeStruct((own_rows, feat), B...  32.1 us
    unnamed x1, local copies, waits for them, and re-layouts  1.36 us

profile of v1, /device:TPU:0, one launch (start us, length us, event | category | flops | bytes accessed | tf_op | source)
XLA Modules:
  0.0 33.5 jit_solution(13037626043066894271)
XLA Ops:
  0.0 32.1 %shard_map.73 = bf16[16,896]{1,0:T(8,128)(2,1)} custom-call(bf16[16,896]{1,0:T(8,128)(2,1)} %tok_ref.1, bf16[896,2,4736]{2,1,0:T(2,128)(2,1)} %gu_ref.1, bf16[4736,896]{1,0:T(8,128)(2,1)} %down_ref.1, bf16[1,16,896]{2,1,0:T(8,128)(2,1)} %bitcast.3, bf16[1,16,896]{2,1,0:T(8,128)(2,1)} %aout_ref.1, s32[2,16]{1,0:T(2,128)} %bitcast.4, f32[2,16]{1,0:T(2,128)} %bitcast.5), custom_call_target="tpu_custom_call" | custom-call | tf_op jit(solution)/shard_map/pallas_call | solution.py:420
  32.1 1.4 %copy.9 = bf16[16,896]{1,0:T(8,128)(2,1)} copy(bf16[16,896]{1,0:T(8,128)(2,1)} %shard_map.73) | data formatting | bytes 57344

commit v2 on v1

--- a/solution.py
+++ b/solution.py
@@ -7,101 +7,33 @@
 from jax.sharding import PartitionSpec as P
 
 LANES = 128
-CHUNK_TILES = 6
-EARLY_CHUNKS = 3
+CHUNK_SHARES = (4, 8, 12, 10, 4)
 MESH = pl.DeviceIdType.MESH
 BF16, F32 = jnp.bfloat16, jnp.float32
 NEAR, FAR = 0, 1
 
-NEAR_READY, FAR_READY = 4.2, 6.0
-LOAD_START, LOAD_TILE = 0.9, 0.135
-DOT_BASE, DOT_TILE = 0.15, 0.083
-DOWN_BASE, DOWN_TILE = 0.12, 0.04
-PARTNER_DELAY, ACROSS_DELAY = 1.05, 2.3
-ACROSS_HALF_TILE = 0.088
+EARLY_STEPS = (
+    ("PN0", "PN1", "RN0", "PN2", "RN1", "PB3", "RN2", "PB4", "PF2", "RN3", "RF3", "RN4", "RF4"),
+    ("AN0", "PF1", "RF2", "AN1", "PF0", "RF1", "RF0", "AN2", "AN3", "AF3", "AN4", "AF4", "LN0"),
+    ("AF2", "LN1", "AF1", "AF0", "DN01", "LN2", "LN3", "LF3", "LN4", "LF4", "DN2", "LF2", "LF1"),
+    ("DN34", "ZN", "LF0", "DF234", "DF01", "ZF"),
+)
+LATE_STEPS = (
+    ("PN0", "PN1", "PN2", "RN0", "RN1", "PF0", "PF1", "RN2", "RF0", "PF2", "RF1", "PB3", "RF2"),
+    ("PB4", "RF3", "RF4", "AF0", "AF1", "RN3", "AF2", "AF3", "AF4", "RN4", "AN0", "AN1", "AN2"),
+    ("LF0", "LF1", "LF2", "DF01", "LF3", "LF4", "AN3", "DF2", "AN4", "DF34", "ZF"),
+    ("LN0", "LN1", "LN2", "DN01", "LN3", "DN2", "LN4", "DN34", "ZN"),
+)
 
 
 def chunks_of(columns):
-    spans, first = [], 0
-    while first < columns:
-        count = min(CHUNK_TILES, columns - first)
-        spans.append((first, count))
-        first += count
+    spans, first, passed = [], 0, 0
+    for share in CHUNK_SHARES:
+        passed += share
+        end = 2 * (columns * passed // (2 * sum(CHUNK_SHARES)))
+        spans.append((first, end - first))
+        first = end
     return spans
-
-
-def plan(spans):
-    count = len(spans)
-    early = min(EARLY_CHUNKS, count)
-    rank = {}
-    for s, chunks in ((NEAR, range(early)), (FAR, range(count)), (NEAR, range(early, count))):
-        for j in chunks:
-            rank[s, j] = len(rank)
-    products = [((NEAR,), j) for j in range(early)] + [((FAR,), j) for j in range(early)]
-    products += [((FAR, NEAR), j) for j in range(early, count)]
-    ready = {}
-    pending_down = [((NEAR, FAR), j) for j in range(early)]
-    pending_down += [((FAR,), j) for j in range(early, count)]
-    pending_down += [((NEAR,), j) for j in range(early, count)]
-    now, link, order = 0.0, 0.0, []
-    loaded = lambda j: LOAD_START + LOAD_TILE * (spans[j][0] + spans[j][1])
-    waiting = []
-
-    def send(j, tiles_half):
-        nonlocal link
-        link = max(link, now) + ACROSS_HALF_TILE * tiles_half
-        return link + ACROSS_DELAY
-
-    far_left = count
-    near_left = count
-    while products or waiting or pending_down:
-        options = []
-        for name, s, j in waiting:
-            options.append((ready[name, s, j], (0 if name != "relay" else 1, rank[s, j]), (name, s, j)))
-        if products:
-            sets, j = products[0]
-            at = max(loaded(j), max(NEAR_READY if s == NEAR else FAR_READY for s in sets))
-            options.append((at, (2, 0), ("product", sets, j)))
-        for sets, j in pending_down:
-            at = [ready.get(("project", s, j)) for s in sets]
-            if None not in at:
-                place = 3 if sets != (FAR,) else 2
-                options.append((max(at), (place, rank[sets[-1], j]), ("project", sets, j)))
-        able = [o for o in options if o[0] <= now + 0.02]
-        pick = min(able, key=lambda o: o[1]) if able else min(options)
-        now = max(now, pick[0])
-        name, s, j = pick[2]
-        order.append(pick[2])
-        half = spans[j][1] / 2
-        if name == "product":
-            products.pop(0)
-            now += DOT_BASE + DOT_TILE * spans[j][1]
-            for one in s:
-                waiting.append(("reduce", one, j))
-                ready["reduce", one, j] = now + PARTNER_DELAY
-        elif name == "project":
-            pending_down.remove((s, j))
-            now += DOWN_BASE + DOWN_TILE * spans[j][1]
-            if FAR in s:
-                far_left -= 1
-                if far_left == 0:
-                    order.append(("finish", FAR, 0))
-            if NEAR in s:
-                near_left -= 1
-                if near_left == 0:
-                    order.append(("finish", NEAR, 0))
-        else:
-            waiting.remove(pick[2])
-            now += 0.03
-            if name == "reduce":
-                waiting.append(("activate", s, j))
-                ready["activate", s, j] = send(j, 2 * half)
-            elif name == "activate":
-                waiting.append(("relay", s, j))
-                ready["relay", s, j] = send(j, half)
-            else:
-                ready["project", s, j] = now + PARTNER_DELAY
-    return order
 
 
 def kernel(
@@ -109,8 +41,8 @@
     gu, down, tok_all, ain_pad, aout_pad, ids, weights, coef_own, coef_all, lhs,
     keep1, send1, recv1, keep2, send2, recv2, hid, total, send_f, recv_f,
     gu_sem, down_sem, in_sem, tok_send, tok_recv, coef_send, coef_recv,
-    s1_send, s1_recv, s2_send, s2_recv, hp_send, hp_recv, hx_send, hx_recv, hr_send, hr_recv,
-    f_send, f_recv,
+    s1_recv, s2_recv, hx_recv, hq_recv, f_recv, s1_send, s2_send, hp_send, hx_send, hr_send,
+    f_send, far_sem,
 ):
     me = lax.axis_index("exp")
     tp = lax.axis_index("tp")
@@ -128,11 +60,17 @@
     far = (me + 2) % 4
     peers = (near, far, (near + 2) % 4)
 
+    late = me // 2
+
     barrier = pltpu.get_barrier_semaphore()
-    for peer in peers:
-        pl.semaphore_signal(barrier, inc=1, device_id={"exp": peer}, device_id_type=MESH)
     for peer in (partner, across):
         pl.semaphore_signal(barrier, inc=1, device_id={"tp": peer}, device_id_type=MESH)
+    pl.semaphore_signal(barrier, inc=1, device_id={"exp": near}, device_id_type=MESH)
+
+    @pl.when(late == 0)
+    def _():
+        for peer in peers[1:]:
+            pl.semaphore_signal(barrier, inc=1, device_id={"exp": peer}, device_id_type=MESH)
 
     in_copies = [
         pltpu.make_async_copy(tok_ref, tok_all.at[me], in_sem.at[0]),
@@ -143,9 +81,18 @@
     ]
     gu_flat = gu_ref.reshape(2 * feat, hidden)
 
-    def gu_copy(t):
+    def gu_copy(t, j):
         cols = pl.ds(pl.multiple_of(t * LANES, LANES), LANES)
-        return pltpu.make_async_copy(gu_flat.at[:, cols], gu.at[t], gu_sem.at[t])
+        return pltpu.make_async_copy(gu_flat.at[:, cols], gu.at[t], gu_sem.at[j])
+
+    def gu_tiles(j):
+        first, count = spans[j]
+        return max(first - 1, 0), first + count - 1
+
+    def gu_wait(j):
+        begin, end = gu_tiles(j)
+        ref = gu.at[pl.ds(begin, end - begin)]
+        pltpu.make_async_copy(ref, ref, gu_sem.at[j]).wait()
 
     def down_rows(j):
         first, count = spans[j]
@@ -159,11 +106,13 @@
     for copy in in_copies:
         copy.start()
 
-    def start_gu(t, carry):
-        gu_copy(t).start()
-        return carry
-
-    lax.fori_loop(0, tiles, start_gu, 0)
+    for j in range(len(spans)):
+
+        def start_gu(t, carry):
+            gu_copy(t, j).start()
+            return carry
+
+        lax.fori_loop(*gu_tiles(j), start_gu, 0)
     for j in range(len(spans)):
         down_copy(j).start()
 
@@ -172,7 +121,7 @@
 
     def exp_copy(src, dst, send, recv, r):
         return pltpu.make_async_remote_copy(
-            src_ref=src, dst_ref=dst, send_sem=send.at[r], recv_sem=recv.at[r],
+            src_ref=src, dst_ref=dst, send_sem=send.at[0], recv_sem=recv.at[r],
             device_id={"exp": peers[r]}, device_id_type=MESH,
         )
 
@@ -180,8 +129,26 @@
         exp_copy(tok_all.at[me], tok_all.at[me], tok_send, tok_recv, r) for r in range(3)
     ]
     coef_copies = [
-        exp_copy(coef_own.at[r], coef_all.at[me], coef_send, coef_recv, r) for r in range(3)
+        exp_copy(
+            coef_own.at[r, pl.ds(0, 1)], coef_all.at[me, pl.ds(0, 1)], coef_send, coef_recv, r
+        )
+        for r in range(3)
     ]
+    pl.semaphore_wait(barrier, 3 + 2 * late)
+
+    @pl.when(late == 1)
+    def _():
+        for peer in peers[1:]:
+            pl.semaphore_signal(far_sem, inc=1, device_id={"exp": peer}, device_id_type=MESH)
+
+    in_copies[0].wait()
+    tok_copies[0].start()
+
+    @pl.when(late == 1)
+    def _():
+        for copy in tok_copies[1:]:
+            copy.start()
+
     in_copies[1].wait()
     in_copies[2].wait()
 
@@ -194,11 +161,12 @@
     for r in range(3):
         coef_own[r, 0:1, :] = coef_line(peers[r])
     coef_all[me, 0:1, :] = coef_line(me)
-    in_copies[0].wait()
-
-    pl.semaphore_wait(barrier, 5)
-    for copy in tok_copies + coef_copies:
-        copy.start()
+    coef_copies[0].start()
+
+    @pl.when(late == 1)
+    def _():
+        for copy in coef_copies[1:]:
+            copy.start()
 
     def span_cols(j):
         first, count = spans[j]
@@ -215,7 +183,7 @@
 
     def tp_copy(src, dst, send, recv, s, j, peer):
         return pltpu.make_async_remote_copy(
-            src_ref=src, dst_ref=dst, send_sem=send.at[s, j], recv_sem=recv.at[s, j],
+            src_ref=src, dst_ref=dst, send_sem=send.at[0], recv_sem=recv.at[s, j],
             device_id={"tp": peer}, device_id_type=MESH,
         )
 
@@ -233,7 +201,7 @@
 
     def hp_copy(s, j):
         ref = hid.at[s, core, :, half_cols(j, side)]
-        return tp_copy(ref, ref, hp_send, hp_recv, s, j, partner)
+        return tp_copy(ref, ref, hp_send, hq_recv, s, j, partner)
 
     def hx_copy(s, j):
         ref = hid.at[s, core, :, half_cols(j, side)]
@@ -241,7 +209,11 @@
 
     def hr_copy(s, j):
         ref = hid.at[s, core, :, half_cols(j, 1 - side)]
-        return tp_copy(ref, ref, hr_send, hr_recv, s, j, partner)
+        return tp_copy(ref, ref, hr_send, hq_recv, s, j, partner)
+
+    def hq_wait(s, j):
+        ref = hid.at[s, 1 - core, :, span_cols(j)]
+        tp_copy(ref, ref, hp_send, hq_recv, s, j, partner).wait_recv()
 
     pair_rows = 2 * own_rows
     row = lax.broadcasted_iota(jnp.int32, (LANES, 4 * LANES), 0)
@@ -284,27 +256,27 @@
 
     arrived = set()
 
-    def product(sets, j):
+    def product(sets, part):
         for s in sets:
             if s not in arrived:
                 arrived.add(s)
                 prepare(s)
-        first, count = spans[j]
-        begin, end = max(first - 1, 0), first + count - 1
-        for t in range(begin, end):
-            if ("gu", t) not in arrived:
-                arrived.add(("gu", t))
-                gu_copy(t).wait()
-        weight = jnp.concatenate([gu[t] for t in range(begin, end)], axis=1)
+        for j in part:
+            if ("gu", j) not in arrived:
+                arrived.add(("gu", j))
+                gu_wait(j)
         rows = slice(0, 4 * pair_rows) if len(sets) == 2 else slice(
             2 * sets[0] * pair_rows, 2 * (sets[0] + 1) * pair_rows
         )
-        value = jnp.dot(lhs[rows, :], weight, preferred_element_type=F32)
-        cols = pl.ds((begin + 1) * LANES, (end - begin) * LANES)
-        for s in sets:
-            at = 2 * s * pair_rows if len(sets) == 2 else 0
-            store_pair(s, cols, value[at:at + 2 * pair_rows])
-            s1_copy(s, j).start()
+        for j in part:
+            begin, end = gu_tiles(j)
+            weight = jnp.concatenate([gu[t] for t in range(begin, end)], axis=1)
+            value = jnp.dot(lhs[rows, :], weight, preferred_element_type=F32)
+            cols = pl.ds((begin + 1) * LANES, (end - begin) * LANES)
+            for s in sets:
+                at = 2 * s * pair_rows if len(sets) == 2 else 0
+                store_pair(s, cols, value[at:at + 2 * pair_rows])
+                s1_copy(s, j).start()
 
     def reduce(s, j):
         s1_copy(s, j).wait_recv()
@@ -321,7 +293,8 @@
         value = jax.nn.silu(pair[:own_rows]) * pair[own_rows:]
         if j == 0:
             first = jnp.where(side == 0, pair[:own_rows, :LANES], value[:, :LANES])
-            value = jnp.concatenate([first, value[:, LANES:]], axis=1)
+            rest = [value[:, LANES:]] if value.shape[1] > LANES else []
+            value = jnp.concatenate([first, *rest], axis=1)
         hid[s, core, :, half_cols(j, side)] = value.astype(BF16)
         hx_copy(s, j).start()
         hp_copy(s, j).start()
@@ -335,7 +308,8 @@
     ) == lax.broadcasted_iota(jnp.int32, (own_rows, own_rows), 1)
 
     def adapter_part(s):
-        if s == NEAR:
+        if "out" not in arrived:
+            arrived.add("out")
             in_copies[4].wait()
         for r in ((0,) if s == NEAR else (1, 2)):
             coef_copies[r].wait_recv()
@@ -347,63 +321,93 @@
             columns.append(jnp.sum(jnp.where(diagonal, line, 0.0), axis=1, keepdims=True))
         return jnp.concatenate(columns, axis=0) * expert_out.astype(F32)
 
-    def project(sets, j):
-        for s in sets:
-            hp_copy(s, j).wait_recv()
-            hr_copy(s, j).wait_recv()
-        if ("down", j) not in arrived:
-            arrived.add(("down", j))
-            down_copy(j).wait()
-        first, count = spans[j]
-        begin, end = max(first, 1), first + count
+    def project(sets, part):
+        for j in part:
+            for s in sets:
+                hq_wait(s, j)
+            if ("down", j) not in arrived:
+                arrived.add(("down", j))
+                down_copy(j).wait()
+        begin, end = max(spans[part[0]][0], 1), spans[part[-1]][0] + spans[part[-1]][1]
         cols = pl.ds(begin * LANES, (end - begin) * LANES)
+        rows = pl.ds((begin - 1) * LANES, (end - begin) * LANES)
         units = jnp.concatenate(
             [hid[s, :, :, cols].reshape(pair_rows, (end - begin) * LANES) for s in sets], axis=0
         )
-        value = jnp.dot(units, down[down_rows(j), :], preferred_element_type=F32)
+        value = jnp.dot(units, down[rows, :], preferred_element_type=F32)
         for i, s in enumerate(sets):
-            part = value[i * pair_rows:(i + 1) * pair_rows]
-            if j == 0:
-                part = part + adapter_part(s)
+            share = value[i * pair_rows:(i + 1) * pair_rows]
+            if part[0] == 0:
+                share = share + adapter_part(s)
             if ("total", s) not in arrived:
                 arrived.add(("total", s))
-                total[s] = part
+                total[s] = share
             else:
-                total[s] += part
-
-    def f_copy(r):
-        return exp_copy(send_f.at[r], recv_f.at[r], f_send, f_recv, r)
-
-    def finish(s, j):
-        for r in ((0,) if s == NEAR else (1, 2)):
-            at = pl.ds(pl.multiple_of(peers[r] % 2 * own_rows, own_rows), own_rows)
+                total[s] += share
+
+    def f_copy(r, peer):
+        return pltpu.make_async_remote_copy(
+            src_ref=send_f.at[r], dst_ref=recv_f.at[r],
+            send_sem=f_send.at[0], recv_sem=f_recv.at[r],
+            device_id={"exp": peer}, device_id_type=MESH,
+        )
+
+    def finish(s, late):
+        if s == NEAR:
+            targets = ((0, near),)
+        elif late:
+            targets = ((me - 1, 0), (4 - me, 1))
+        else:
+            targets = ((1, peers[1]), (2, peers[2]))
+        for r, peer in targets:
+            at = pl.ds(pl.multiple_of(peer % 2 * own_rows, own_rows), own_rows)
             send_f[r] = total[s, at, :].astype(BF16)
-            f_copy(r).start()
-
-    stages = {
-        "product": product, "reduce": reduce, "activate": activate, "relay": relay,
-        "project": project, "finish": finish,
-    }
-    for name, s, j in plan(spans):
-        with jax.named_scope(f"{name}{s}{j}"):
-            stages[name](s, j)
+            f_copy(r, peer).start()
+
+    single = {"R": reduce, "A": activate, "L": relay}
+    sets_of = {"N": (NEAR,), "F": (FAR,), "B": (FAR, NEAR)}
+
+    def run(which):
+        arrived.clear()
+        if not which:
+            with jax.named_scope("open"):
+                pl.semaphore_wait(far_sem, 2)
+                for copy in tok_copies[1:] + coef_copies[1:]:
+                    copy.start()
+        for step in sum(LATE_STEPS if which else EARLY_STEPS, ()):
+            kind, sets, part = step[0], sets_of[step[1]], tuple(int(c) for c in step[2:])
+            with jax.named_scope(step):
+                if kind == "Z":
+                    finish(sets[0], which)
+                elif kind == "D":
+                    project(sets, part)
+                elif kind == "P":
+                    product(sets, part)
+                else:
+                    single[kind](sets[0], part[0])
+
+    for which in range(2):
+        pl.when(late == which)(functools.partial(run, which))
 
     with jax.named_scope("sends"):
-        for copy in tok_copies + coef_copies:
-            copy.wait_send()
-        for s in range(2):
-            for j in range(len(spans)):
-                for make in (s1_copy, s2_copy, hp_copy, hx_copy, hr_copy):
-                    make(s, j).wait_send()
+        exp_copy(
+            tok_all.at[pl.ds(0, 3)], tok_all.at[pl.ds(0, 3)], tok_send, tok_recv, 0
+        ).wait_send()
+        line = coef_own.at[:, pl.ds(0, 1)]
+        exp_copy(line, line, coef_send, coef_recv, 0).wait_send()
+        tp_copy(send1, recv1, s1_send, s1_recv, 0, 0, partner).wait_send()
+        tp_copy(send2, recv2, s2_send, s2_recv, 0, 0, across).wait_send()
+        part = hid.at[:, 0, :, pl.ds(0, (tiles + 1) // 2 * LANES)]
+        for send in (hp_send, hx_send, hr_send):
+            tp_copy(part, part, send, hx_recv, 0, 0, across).wait_send()
     own = pl.ds(pl.multiple_of(me % 2 * own_rows, own_rows), own_rows)
     result = total[NEAR, own, :]
     for r in (1, 2, 0):
         with jax.named_scope(f"final{r}"):
-            f_copy(r).wait_recv()
+            f_copy(r, peers[r]).wait_recv()
         result = result + recv_f[r].astype(F32)
     out_ref[...] = result.astype(out_ref.dtype)
-    for r in range(3):
-        f_copy(r).wait_send()
+    exp_copy(send_f, recv_f, f_send, f_recv, 0).wait_send()
 
 
 def fused(tokens, gate_up_weight, down_weight, adapter_in, adapter_out, expert_ids, route_weight):
@@ -419,7 +423,7 @@
     pair = 2 * own_rows
     return pl.pallas_call(
         kernel,
-        out_shape=jax.ShapeDtypeStruct((own_rows, feat), BF16),
+        out_shape=pltpu.VMEM((own_rows, feat), BF16),
         in_specs=[in_place] * 7,
         out_specs=pl.BlockSpec(memory_space=pltpu.VMEM),
         scratch_shapes=[
@@ -443,10 +447,11 @@
             vmem((2, pair, feat), F32),
             vmem((3, own_rows, feat), BF16),
             vmem((3, own_rows, feat), BF16),
-            dma(tiles), dma(chunk_count), dma(5),
-            dma(3), dma(3), dma(3), dma(3),
-            *[dma(2, chunk_count) for _ in range(10)],
-            dma(3), dma(3),
+            dma(chunk_count), dma(chunk_count), dma(5),
+            dma(1), dma(3), dma(1), dma(3),
+            *[dma(2, chunk_count) for _ in range(4)],
+            dma(3), *[dma(1) for _ in range(6)],
+            pltpu.SemaphoreType.REGULAR,
         ],
         compiler_params=pltpu.CompilerParams(
             collective_id=0, has_side_effects=True, vmem_limit_bytes=60 * 2**20
@@ -534,6 +539,7 @@
         and own_rows % 16 == 0
         and feat % LANES == 0
         and gate_up_weight.shape[2] % (2 * LANES) == LANES
+        and gate_up_weight.shape[2] >= 19 * LANES
     )
     return (fused if fits else plain)(tokens, gate_up_weight, *rest)
 

time: 33.7 us -> 28.9 us (0.86)
  the two profiles are of different devices: /device:TPU:0 before, /device:TPU:17 now
where the time goes in v2:
time: 28.9 us; the launch traced here: 28.8 us
  Pallas kernels  28.2 us (98%)
  local copies, waits for them, and re-layouts  0.61 us (2%)
    pallas_call x1, Pallas kernels, fused(): pl.pallas_call(kernel, out_shape=pltpu.VMEM((own_rows, feat), BF16), in_s...  28.2 us
    unnamed x1, local copies, waits for them, and re-layouts  0.61 us

profile of v2, /device:TPU:17, one launch (start us, length us, event | category | flops | bytes accessed | tf_op | source)
XLA Modules:
  0.0 28.8 jit_solution(3298876732301676044)
XLA Ops:
  0.0 28.2 %shard_map.73 = bf16[16,896]{1,0:T(8,128)(2,1)S(1)} custom-call(bf16[16,896]{1,0:T(8,128)(2,1)} %tok_ref.1, bf16[896,2,4736]{2,1,0:T(2,128)(2,1)} %gu_ref.1, bf16[4736,896]{1,0:T(8,128)(2,1)} %down_ref.1, bf16[1,16,896]{2,1,0:T(8,128)(2,1)} %bitcast.3, bf16[1,16,896]{2,1,0:T(8,128)(2,1)} %aout_ref.1, s32[2,16]{1,0:T(2,128)} %bitcast.4, f32[2,16]{1,0:T(2,128)} %bitcast.5), custom_call_target="tpu_custom_call" | custom-call | tf_op jit(solution)/shard_map/pallas_call | solution.py:424
  28.2 0.6 %copy.9 = bf16[16,896]{1,0:T(8,128)(2,1)} copy(bf16[16,896]{1,0:T(8,128)(2,1)S(1)} %shard_map.73) | data formatting | bytes 57344

commit v3 on v2

--- a/solution.py
+++ b/solution.py
@@ -8,6 +8,7 @@
 
 LANES = 128
 CHUNK_SHARES = (4, 8, 12, 10, 4)
+PIECE_OF = (0, 0, 1, 2, 2)
 MESH = pl.DeviceIdType.MESH
 BF16, F32 = jnp.bfloat16, jnp.float32
 NEAR, FAR = 0, 1
@@ -16,13 +17,13 @@
     ("PN0", "PN1", "RN0", "PN2", "RN1", "PB3", "RN2", "PB4", "PF2", "RN3", "RF3", "RN4", "RF4"),
     ("AN0", "PF1", "RF2", "AN1", "PF0", "RF1", "RF0", "AN2", "AN3", "AF3", "AN4", "AF4", "LN0"),
     ("AF2", "LN1", "AF1", "AF0", "DN01", "LN2", "LN3", "LF3", "LN4", "LF4", "DN2", "LF2", "LF1"),
-    ("DN34", "ZN", "LF0", "DF234", "DF01", "ZF"),
+    ("LF0", "DB34", "ZN", "DF2", "DF01", "ZF"),
 )
 LATE_STEPS = (
     ("PN0", "PN1", "PN2", "RN0", "RN1", "PF0", "PF1", "RN2", "RF0", "PF2", "RF1", "PB3", "RF2"),
-    ("PB4", "RF3", "RF4", "AF0", "AF1", "RN3", "AF2", "AF3", "AF4", "RN4", "AN0", "AN1", "AN2"),
-    ("LF0", "LF1", "LF2", "DF01", "LF3", "LF4", "AN3", "DF2", "AN4", "DF34", "ZF"),
-    ("LN0", "LN1", "LN2", "DN01", "LN3", "DN2", "LN4", "DN34", "ZN"),
+    ("PB4", "RF3", "RF4", "AF0", "AF1", "RN3", "AF2", "RN4", "AF3", "AF4", "AN0", "AN1", "AN2"),
+    ("LF0", "LF1", "AN3", "LF2", "DF01", "LF3", "LF4", "AN4", "DF2", "LN0", "LN1", "DF34", "ZF"),
+    ("LN2", "DN01", "LN3", "LN4", "DN2", "DN34", "ZN"),
 )
 
 
@@ -42,7 +43,7 @@
     keep1, send1, recv1, keep2, send2, recv2, hid, total, send_f, recv_f,
     gu_sem, down_sem, in_sem, tok_send, tok_recv, coef_send, coef_recv,
     s1_recv, s2_recv, hx_recv, hq_recv, f_recv, s1_send, s2_send, hp_send, hx_send, hr_send,
-    f_send, far_sem,
+    f_send, met_sem,
 ):
     me = lax.axis_index("exp")
     tp = lax.axis_index("tp")
@@ -61,16 +62,20 @@
     peers = (near, far, (near + 2) % 4)
 
     late = me // 2
-
     barrier = pltpu.get_barrier_semaphore()
-    for peer in (partner, across):
-        pl.semaphore_signal(barrier, inc=1, device_id={"tp": peer}, device_id_type=MESH)
-    pl.semaphore_signal(barrier, inc=1, device_id={"exp": near}, device_id_type=MESH)
-
-    @pl.when(late == 0)
-    def _():
-        for peer in peers[1:]:
-            pl.semaphore_signal(barrier, inc=1, device_id={"exp": peer}, device_id_type=MESH)
+
+    def tell(condition, semaphore, axis, *targets):
+        @pl.when(condition)
+        def _():
+            for peer in targets:
+                pl.semaphore_signal(
+                    semaphore, inc=1, device_id={axis: peer}, device_id_type=MESH
+                )
+
+    tell(late == 0, barrier, "exp", *peers[1:])
+    tell(me >= 0, barrier, "exp", near)
+    tell(side == 0, barrier, "tp", across)
+    tell(core == 1, barrier, "tp", partner)
 
     in_copies = [
         pltpu.make_async_copy(tok_ref, tok_all.at[me], in_sem.at[0]),
@@ -94,14 +99,7 @@
         ref = gu.at[pl.ds(begin, end - begin)]
         pltpu.make_async_copy(ref, ref, gu_sem.at[j]).wait()
 
-    def down_rows(j):
-        first, count = spans[j]
-        begin, end = max(first - 1, 0), first + count - 1
-        return pl.ds(begin * LANES, (end - begin) * LANES)
-
-    def down_copy(j):
-        rows = down_rows(j)
-        return pltpu.make_async_copy(down_ref.at[rows], down.at[rows], down_sem.at[j])
+    down_copy = pltpu.make_async_copy(down_ref, down, down_sem.at[0])
 
     for copy in in_copies:
         copy.start()
@@ -113,8 +111,7 @@
             return carry
 
         lax.fori_loop(*gu_tiles(j), start_gu, 0)
-    for j in range(len(spans)):
-        down_copy(j).start()
+    down_copy.start()
 
     ain_pad[rank:, :] = jnp.zeros((LANES - rank, feat), BF16)
     aout_pad[rank:, :] = jnp.zeros((LANES - rank, feat), BF16)
@@ -134,20 +131,20 @@
         )
         for r in range(3)
     ]
-    pl.semaphore_wait(barrier, 3 + 2 * late)
-
-    @pl.when(late == 1)
-    def _():
-        for peer in peers[1:]:
-            pl.semaphore_signal(far_sem, inc=1, device_id={"exp": peer}, device_id_type=MESH)
-
+    pl.semaphore_wait(barrier, 2 * late + side + 2 - core)
+    tell(late == 1, met_sem.at[0], "exp", *peers[1:])
+    tell(side == 1, met_sem.at[1], "tp", across)
+    tell(core == 0, met_sem.at[2], "tp", partner)
     in_copies[0].wait()
+
+    def send_far(condition):
+        @pl.when(condition)
+        def _():
+            for copy in tok_copies[1:]:
+                copy.start()
+
     tok_copies[0].start()
-
-    @pl.when(late == 1)
-    def _():
-        for copy in tok_copies[1:]:
-            copy.start()
+    send_far(late == 1)
 
     in_copies[1].wait()
     in_copies[2].wait()
@@ -168,6 +165,15 @@
         for copy in coef_copies[1:]:
             copy.start()
 
+    @pl.when(side == 0)
+    def _():
+        pl.semaphore_wait(met_sem.at[1], 1)
+
+    @pl.when(core == 1)
+    def _():
+        pl.semaphore_wait(met_sem.at[2], 1)
+
+
     def span_cols(j):
         first, count = spans[j]
         return pl.ds(first * LANES, count * LANES)
@@ -201,7 +207,7 @@
 
     def hp_copy(s, j):
         ref = hid.at[s, core, :, half_cols(j, side)]
-        return tp_copy(ref, ref, hp_send, hq_recv, s, j, partner)
+        return tp_copy(ref, ref, hp_send, hq_recv, s, PIECE_OF[j], partner)
 
     def hx_copy(s, j):
         ref = hid.at[s, core, :, half_cols(j, side)]
@@ -209,11 +215,13 @@
 
     def hr_copy(s, j):
         ref = hid.at[s, core, :, half_cols(j, 1 - side)]
-        return tp_copy(ref, ref, hr_send, hq_recv, s, j, partner)
-
-    def hq_wait(s, j):
-        ref = hid.at[s, 1 - core, :, span_cols(j)]
-        tp_copy(ref, ref, hp_send, hq_recv, s, j, partner).wait_recv()
+        return tp_copy(ref, ref, hr_send, hq_recv, s, PIECE_OF[j], partner)
+
+    def hq_wait(s, piece):
+        members = [j for j in range(len(spans)) if PIECE_OF[j] == piece]
+        first, (last, count) = spans[members[0]][0], spans[members[-1]]
+        ref = hid.at[s, 1 - core, :, pl.ds(first * LANES, (last + count - first) * LANES)]
+        tp_copy(ref, ref, hp_send, hq_recv, s, piece, partner).wait_recv()
 
     pair_rows = 2 * own_rows
     row = lax.broadcasted_iota(jnp.int32, (LANES, 4 * LANES), 0)
@@ -322,12 +330,12 @@
         return jnp.concatenate(columns, axis=0) * expert_out.astype(F32)
 
     def project(sets, part):
-        for j in part:
+        for piece in sorted({PIECE_OF[j] for j in part}):
             for s in sets:
-                hq_wait(s, j)
-            if ("down", j) not in arrived:
-                arrived.add(("down", j))
-                down_copy(j).wait()
+                hq_wait(s, piece)
+        if "down" not in arrived:
+            arrived.add("down")
+            down_copy.wait()
         begin, end = max(spans[part[0]][0], 1), spans[part[-1]][0] + spans[part[-1]][1]
         cols = pl.ds(begin * LANES, (end - begin) * LANES)
         rows = pl.ds((begin - 1) * LANES, (end - begin) * LANES)
@@ -371,7 +379,7 @@
         arrived.clear()
         if not which:
             with jax.named_scope("open"):
-                pl.semaphore_wait(far_sem, 2)
+                pl.semaphore_wait(met_sem.at[0], 2)
                 for copy in tok_copies[1:] + coef_copies[1:]:
                     copy.start()
         for step in sum(LATE_STEPS if which else EARLY_STEPS, ()):
@@ -447,11 +455,11 @@
             vmem((2, pair, feat), F32),
             vmem((3, own_rows, feat), BF16),
             vmem((3, own_rows, feat), BF16),
-            dma(chunk_count), dma(chunk_count), dma(5),
+            dma(chunk_count), dma(1), dma(5),
             dma(1), dma(3), dma(1), dma(3),
-            *[dma(2, chunk_count) for _ in range(4)],
+            *[dma(2, chunk_count) for _ in range(3)], dma(2, PIECE_OF[-1] + 1),
             dma(3), *[dma(1) for _ in range(6)],
-            pltpu.SemaphoreType.REGULAR,
+            pltpu.SemaphoreType.REGULAR((3,)),
         ],
         compiler_params=pltpu.CompilerParams(
             collective_id=0, has_side_effects=True, vmem_limit_bytes=60 * 2**20

time: 28.9 us -> 28.4 us (0.983)
  the two profiles are of different devices: /device:TPU:17 before, /device:TPU:0 now
where the time goes in v3:
time: 28.4 us; the launch traced here: 28.3 us
  Pallas kernels  27.7 us (98%)
  local copies, waits for them, and re-layouts  0.61 us (2%)
    pallas_call x1, Pallas kernels, fused(): pl.pallas_call(kernel, out_shape=pltpu.VMEM((own_rows, feat), BF16), in_s...  27.7 us
    unnamed x1, local copies, waits for them, and re-layouts  0.61 us

profile of v3, /device:TPU:0, one launch (start us, length us, event | category | flops | bytes accessed | tf_op | source)
XLA Modules:
  0.0 28.3 jit_solution(12991280580978836208)
XLA Ops:
  0.0 27.7 %shard_map.73 = bf16[16,896]{1,0:T(8,128)(2,1)S(1)} custom-call(bf16[16,896]{1,0:T(8,128)(2,1)} %tok_ref.1, bf16[896,2,4736]{2,1,0:T(2,128)(2,1)} %gu_ref.1, bf16[4736,896]{1,0:T(8,128)(2,1)} %down_ref.1, bf16[1,16,896]{2,1,0:T(8,128)(2,1)} %bitcast.3, bf16[1,16,896]{2,1,0:T(8,128)(2,1)} %aout_ref.1, s32[2,16]{1,0:T(2,128)} %bitcast.4, f32[2,16]{1,0:T(2,128)} %bitcast.5), custom_call_target="tpu_custom_call" | custom-call | tf_op jit(solution)/shard_map/pallas_call | solution.py:432
  27.7 0.6 %copy.9 = bf16[16,896]{1,0:T(8,128)(2,1)} copy(bf16[16,896]{1,0:T(8,128)(2,1)S(1)} %shard_map.73) | data formatting | bytes 57344

commit v4 on v3

--- a/solution.py
+++ b/solution.py
@@ -20,9 +20,9 @@
     ("LF0", "DB34", "ZN", "DF2", "DF01", "ZF"),
 )
 LATE_STEPS = (
-    ("PN0", "PN1", "PN2", "RN0", "RN1", "PF0", "PF1", "RN2", "RF0", "PF2", "RF1", "PB3", "RF2"),
-    ("PB4", "RF3", "RF4", "AF0", "AF1", "RN3", "AF2", "RN4", "AF3", "AF4", "AN0", "AN1", "AN2"),
-    ("LF0", "LF1", "AN3", "LF2", "DF01", "LF3", "LF4", "AN4", "DF2", "LN0", "LN1", "DF34", "ZF"),
+    ("PN0", "PN1", "PN2", "RN0", "RN1", "PF2", "RN2", "PF1", "PF0", "RF2", "PB3", "RF1", "RF0"),
+    ("PB4", "RF3", "RF4", "RN3", "AF2", "AF1", "AF0", "RN4", "AF3", "AF4", "AN0", "AN1", "AN2"),
+    ("LF2", "AN3", "LF1", "LF0", "DF2", "LF3", "LF4", "AN4", "DF01", "LN0", "LN1", "DF34", "ZF"),
     ("LN2", "DN01", "LN3", "LN4", "DN2", "DN34", "ZN"),
 )
 

time: 28.4 us -> 28.5 us (level)
  no operation moved by 1% of the time
where the time goes in v4:
time: 28.5 us; the launch traced here: 28.4 us
  Pallas kernels  27.7 us (97%)
  local copies, waits for them, and re-layouts  0.61 us (2%)
    pallas_call x1, Pallas kernels, fused(): pl.pallas_call(kernel, out_shape=pltpu.VMEM((own_rows, feat), BF16), in_s...  27.7 us
    unnamed x1, local copies, waits for them, and re-layouts  0.61 us

profile of v4, /device:TPU:0, one launch (start us, length us, event | category | flops | bytes accessed | tf_op | source)
XLA Modules:
  0.0 28.4 jit_solution(4243010266236795203)
XLA Ops:
  0.0 27.7 %shard_map.73 = bf16[16,896]{1,0:T(8,128)(2,1)S(1)} custom-call(bf16[16,896]{1,0:T(8,128)(2,1)} %tok_ref.1, bf16[896,2,4736]{2,1,0:T(2,128)(2,1)} %gu_ref.1, bf16[4736,896]{1,0:T(8,128)(2,1)} %down_ref.1, bf16[1,16,896]{2,1,0:T(8,128)(2,1)} %bitcast.3, bf16[1,16,896]{2,1,0:T(8,128)(2,1)} %aout_ref.1, s32[2,16]{1,0:T(2,128)} %bitcast.4, f32[2,16]{1,0:T(2,128)} %bitcast.5), custom_call_target="tpu_custom_call" | custom-call | tf_op jit(solution)/shard_map/pallas_call | solution.py:432
  27.7 0.6 %copy.9 = bf16[16,896]{1,0:T(8,128)(2,1)} copy(bf16[16,896]{1,0:T(8,128)(2,1)S(1)} %shard_map.73) | data formatting | bytes 57344
